TPU v7x, 32 devices: a whole 2x2x4 slice. The times are simulated.
32 devices in a mesh: blk: 8 (over y, x, core), wide: 4 (over z).
Axes of the slice: x: 2, y: 2, z: 4, core: 2. Of those that a mesh axis runs over, the one named last changes fastest.
Arguments:
- points: bfloat16 [8192, 32], P(('blk', 'wide')), may hold values from -6 to 6
- inv_length: float32 [32], replicated, may hold values from 0.2 to 0.7
- noise_var: float32 [], replicated, may hold values from 0.1 to 1
- solution: float32 [8192, 128], P(('blk', 'wide')), may hold values from -6 to 6
- residual: float32 [8192, 128], P(('blk', 'wide')), may hold values from -6 to 6
- direction: float32 [8192, 128], P(('blk', 'wide')), may hold values from -6 to 6
Outputs:
- new_solution: float32 [8192, 128], P(('blk', 'wide'))
- new_residual: float32 [8192, 128], P(('blk', 'wide'))
- new_direction: float32 [8192, 128], P(('blk', 'wide'))
All inputs are finite; a program needn't handle non-finite values.
Results may differ from a plain program's by a relative error of at most 0.01.
Values may be sent and summed in bfloat16 or wider, within the bound.
A program may use at most 64 MiB of HBM per device.

v0:
```python
import functools
import math

import jax
import jax.numpy as jnp
from jax import lax
from jax.experimental import pallas as pl
from jax.experimental.pallas import tpu as pltpu
from jax.sharding import PartitionSpec as P

LN2 = math.log(2.0)
SCALE = 5.0 / (LN2 * LN2)
MESH = pl.DeviceIdType.MESH
TAIL = 16


def rounded(x):
    return x.astype(jnp.bfloat16).astype(jnp.float32)


def three_parts(x):
    high = rounded(x)
    rest = x - high
    middle = rounded(rest)
    return high, middle, rounded(rest - middle)


def matern(scaled_dist):
    dist = jnp.maximum(scaled_dist, 1e-30)
    root = dist * lax.rsqrt(dist)
    poly = 1.0 + root * (LN2 + (LN2 * LN2 / 3.0) * root)
    return (poly * jnp.exp2(-root)).astype(jnp.bfloat16)


def kernel(nb, nw, points_in, inv_in, noise_in, residual_in, direction_in, image_out, step_out, ratio_out,
           points, inv_length, noise_var, residual, direction, image, io, feat, feat_z, rows_x, kmat, low_dir, part, part_in, stat, stat_z, stat_b, stat_o,
           fs, fr, fzs, fzr, ps, pr, qs, qr, zs, zr, bs, br):
    b = lax.axis_index("blk")
    w = lax.axis_index("wide")
    chips = nb // 2
    chip, core = b // 2, b % 2
    features, piece = points.shape

    def same_core(q):
        return (lax.rem(chip + q, chips) * 2 + core, w)

    sibling = (chip * 2 + 1 - core, w)

    def along(q):
        return (b, lax.rem(w + q, nw))

    def plane(slot):
        return (lax.rem(chip + slot // 2, chips) * 2 + (core if slot % 2 == 0 else 1 - core), w)

    def back(slot):
        return (chips - slot // 2) % chips * 2 + slot % 2

    barrier = pltpu.get_barrier_semaphore()
    for slot in range(1, nb):
        pl.semaphore_signal(barrier, inc=1, device_id=plane(slot), device_id_type=MESH)
    for q in range(1, nw):
        pl.semaphore_signal(barrier, inc=1, device_id=along(q), device_id_type=MESH)

    def copy(src, dst, send, recv, to):
        return pltpu.make_async_remote_copy(
            src_ref=src, dst_ref=dst, send_sem=send, recv_sem=recv, device_id=to, device_id_type=MESH
        )

    loads = [
        pltpu.make_async_copy(src, dst, io.at[k])
        for k, (src, dst) in enumerate(
            ((points_in, points), (inv_in, inv_length), (direction_in, direction),
             (noise_in, noise_var), (residual_in, residual))
        )
    ]
    for load in loads:
        load.start()
    for load in loads[:2]:
        load.wait()

    inv_row = jnp.concatenate(
        [inv_length[...], jnp.zeros((1, 128 - features), jnp.float32)], axis=1)
    inv_column = jnp.broadcast_to(inv_row, (8, 128)).T[:features, 0:1]
    x_t = rounded(points[...].astype(jnp.float32) * inv_column)
    s1, s2, s3 = three_parts(SCALE * jnp.sum(x_t * x_t, axis=0, keepdims=True))
    row = lax.broadcasted_iota(jnp.int32, (TAIL, piece), 0)
    tail = jnp.where((row >= 3) & (row <= 10), 1.0, 0.0)
    tail = jnp.where((row >= 6) & (row <= 7), 0.0, tail)
    for at, value in ((0, s1), (1, s2), (2, s3), (11, s1), (12, s2), (13, s3)):
        tail = jnp.where(row == at, value, tail)
    feat[0] = jnp.concatenate([x_t, tail], axis=0).astype(jnp.bfloat16)
    for load in loads[2:]:
        load.wait()
    low_dir[0:piece] = direction[...].astype(jnp.bfloat16)
    pl.semaphore_wait(barrier, nb - 1 + nw - 1)

    upper = lax.div(2 * w, nw)

    def near(k):
        return k + upper * (nw - 2 * k)

    def rows_at(q):
        return pl.ds(pl.multiple_of(q * piece, piece), piece)

    sends = []

    def go(c):
        c.start()
        sends.append(c)
        return c

    def feat_copy(src_slot, dst_slot, to):
        return copy(feat.at[src_slot], feat.at[dst_slot], fs.at[dst_slot], fr.at[dst_slot], to)

    def dir_copy(src_slot, dst_slot, to):
        return copy(low_dir.at[pl.ds(src_slot * piece, piece)], low_dir.at[pl.ds(dst_slot * piece, piece)],
                    ps.at[dst_slot], pr.at[dst_slot], to)

    for k in range(1, nw):
        q = near(nw - k)
        go(copy(feat.at[0], feat_z.at[nw - q], fzs.at[q], fzr.at[nw - q], along(q)))
    go(feat_copy(0, 1, sibling))
    for q in range(1, chips):
        go(feat_copy(0, 2 * (chips - q), same_core(q)))
    for q in range(1, chips):
        go(dir_copy(0, 2 * (chips - q), same_core(q)))
    go(dir_copy(0, 1, sibling))

    def feat_arrived(slot):
        feat_copy(slot, slot, sibling).wait_recv()

    def dir_arrived(slot):
        dir_copy(slot, slot, sibling).wait_recv()

    def as_rows(block):
        block = block.astype(jnp.float32)
        x = block[:features]
        h, m, l = three_parts(SCALE * x)
        lanes = jnp.concatenate(
            [-2.0 * h, -2.0 * m, -2.0 * l, block[features + 8 :],
             jnp.zeros((TAIL + 8, piece), jnp.float32)], axis=0)
        return lanes.T.astype(jnp.bfloat16)

    depth = rows_x.shape[1]

    def tile(at, slot):
        block = feat[slot]
        cols = jnp.concatenate(
            [block[:features]] * 3 + [block[features:],
             jnp.zeros((depth - 3 * features - TAIL, piece), jnp.bfloat16)], axis=0)
        dist = jnp.dot(rows_x[at, :], cols, preferred_element_type=jnp.float32)
        kmat[at, slot * piece : (slot + 1) * piece] = matern(dist)

    def feat_z_arrived(q):
        copy(feat_z.at[q], feat_z.at[q], fzs.at[q], fzr.at[q], along(q)).wait_recv()

    def relay_direction(q):
        dir_arrived(2 * q)
        go(dir_copy(2 * q, 2 * q + 1, sibling))

    rows_x[0:piece] = as_rows(feat[0])
    tile(pl.ds(0, piece), 0)
    feat_arrived(1)
    tile(pl.ds(0, piece), 1)
    for q in range(1, chips):
        feat_arrived(2 * q)
        go(feat_copy(2 * q, 2 * q + 1, sibling))
        tile(pl.ds(0, piece), 2 * q)
    for q in range(1, chips):
        feat_arrived(2 * q + 1)
        tile(pl.ds(0, piece), 2 * q + 1)
    if nw <= 4:
        relayed = 1
        for k in range(1, nw):
            q = near(k)
            feat_z_arrived(q)
            rows_x[rows_at(q), :] = as_rows(feat_z[q])
            for slot in range(nb):
                tile(rows_at(q), slot)
                if k == nw - 1 and slot in (0, nb // 2) and relayed < chips:
                    relay_direction(relayed)
                    relayed += 1
    else:
        relayed = 1
        for q in range(1, nw):
            feat_z_arrived(q)
            rows_x[q * piece : (q + 1) * piece] = as_rows(feat_z[q])

        def row_tiles(q, carry):
            for slot in range(nb):
                tile(pl.ds(pl.multiple_of(q * piece, piece), piece), slot)
            return carry

        lax.fori_loop(1, nw, row_tiles, 0)
    for q in range(relayed, chips):
        relay_direction(q)
    for q in range(chips):
        dir_arrived(2 * q + 1)

    def partial(q):
        return jnp.dot(kmat[rows_at(q), :], low_dir[...],
                       preferred_element_type=jnp.float32)

    for k in range(1, nw):
        q = near(nw - k)
        part[q] = partial(q).astype(jnp.bfloat16)
        go(copy(part.at[q], part_in.at[nw - q], qs.at[q], qr.at[nw - q], along(q)))
    total = partial(0) + noise_var[...] * direction[...]
    for q in range(1, nw):
        copy(part.at[q], part_in.at[q], qs.at[q], qr.at[q], along(q)).wait_recv()
        total = total + part_in[q].astype(jnp.float32)
    image[...] = total
    store = pltpu.make_async_copy(image, image_out, io.at[5])
    store.start()

    def column_sum(x):
        return jnp.sum(x, axis=0, keepdims=True)

    res, direc = residual[...], direction[...]
    at = lax.broadcasted_iota(jnp.int32, (8, res.shape[1]), 0)
    sums = jnp.zeros(at.shape, jnp.float32)
    for k, value in enumerate((res * res, direc * total, res * total, total * total)):
        sums = jnp.where(at == k, column_sum(value), sums)
    stat[...] = sums
    for q in range(1, nw):
        go(copy(stat, stat_z.at[nw - q], zs.at[q], zr.at[nw - q], along(q)))
    for q in range(1, nw):
        copy(stat, stat_z.at[q], zs.at[q], zr.at[q], along(q)).wait_recv()
        sums = sums + stat_z[q]
    stat_o[...] = sums
    for slot in range(1, nb):
        go(copy(stat_o, stat_b.at[back(slot)], bs.at[slot], br.at[back(slot)], plane(slot)))
    for slot in range(1, nb):
        copy(stat_o, stat_b.at[slot], bs.at[slot], br.at[slot], plane(slot)).wait_recv()
        sums = sums + stat_b[slot]
    old_norm, step = sums[0:1], sums[0:1] / sums[1:2]
    new_norm = old_norm - 2.0 * step * sums[2:3] + step * step * sums[3:4]
    step_out[...] = step
    ratio_out[...] = new_norm / old_norm
    store.wait()
    for c in sends:
        c.wait_send()


def on_device(nb, nw, points, inv_length, noise_var, solution, residual, direction):
    piece, features = points.shape
    rhs = direction.shape[1]
    vmem = pl.BlockSpec(memory_space=pltpu.VMEM)
    hbm = pl.BlockSpec(memory_space=pl.ANY)
    dma = pltpu.SemaphoreType.DMA
    depth = 3 * features + 2 * TAIL
    image, step_length, ratio = pl.pallas_call(
        functools.partial(kernel, nb, nw),
        out_shape=(
            jax.ShapeDtypeStruct((piece, rhs), jnp.float32),
            jax.ShapeDtypeStruct((1, rhs), jnp.float32),
            jax.ShapeDtypeStruct((1, rhs), jnp.float32),
        ),
        in_specs=[hbm] * 5,
        out_specs=(hbm, vmem, vmem),
        scratch_shapes=[
            pltpu.VMEM((features, piece), points.dtype),
            pltpu.VMEM((1, features), jnp.float32),
            pltpu.VMEM((1, 1), jnp.float32),
            pltpu.VMEM((piece, rhs), jnp.float32),
            pltpu.VMEM((piece, rhs), jnp.float32),
            pltpu.VMEM((piece, rhs), jnp.float32),
            dma((6,)),
            pltpu.VMEM((nb, features + TAIL, piece), jnp.bfloat16),
            pltpu.VMEM((nw, features + TAIL, piece), jnp.bfloat16),
            pltpu.VMEM((nw * piece, depth), jnp.bfloat16),
            pltpu.VMEM((nw * piece, nb * piece), jnp.bfloat16),
            pltpu.VMEM((nb * piece, rhs), jnp.bfloat16),
            pltpu.VMEM((nw, piece, rhs), jnp.bfloat16),
            pltpu.VMEM((nw, piece, rhs), jnp.bfloat16),
            pltpu.VMEM((8, rhs), jnp.float32),
            pltpu.VMEM((nw, 8, rhs), jnp.float32),
            pltpu.VMEM((nb, 8, rhs), jnp.float32),
            pltpu.VMEM((8, rhs), jnp.float32),
            dma((nb,)), dma((nb,)), dma((nw,)), dma((nw,)), dma((nb,)), dma((nb,)),
            dma((nw,)), dma((nw,)), dma((nw,)), dma((nw,)), dma((nb,)), dma((nb,)),
        ],
        compiler_params=pltpu.CompilerParams(
            collective_id=0, has_side_effects=True, vmem_limit_bytes=60 * 1024 * 1024
        ),
    )(points.T, inv_length.reshape(1, features), noise_var.reshape(1, 1), residual, direction)
    new_residual = residual - step_length * image
    new_solution = solution + step_length * direction
    new_direction = new_residual + ratio * direction
    return (new_solution, new_residual, new_direction)


def solution(mesh):
    spec = P(("blk", "wide"), None)
    return jax.shard_map(
        functools.partial(on_device, mesh.shape["blk"], mesh.shape["wide"]),
        mesh=mesh,
        in_specs=(spec, P(), P(), spec, spec, spec),
        out_specs=(spec, spec, spec),
        check_vma=False,
    )
```

profile of v0, /device:TPU:0, one launch (start us, length us, event | category | flops | bytes accessed | tf_op | source)
XLA Modules:
  0.0 34.7 jit_solution(9100170816936021639)
XLA Ops:
  1.3 0.0 copy-start
  1.3 0.0 copy-start.1
  1.3 31.0 %shard_map.85 = (f32[256,128]{1,0:T(8,128)}, f32[1,128]{1,0:T(1,128)}, f32[1,128]{1,0:T(1,128)}) custom-call(bf16[32,256]{1,0:T(8,128)(2,1)} %bitcast.6, f32[1,32]{1,0:T(1,128)} %bitcast.7, f32[1,1]{1,0:T(1,128)} %bitcast.5.noise_in, f32[256,128]{1,0:T(8,128)} %residual_in.1, f32[256,128]{1,0:T(8,128)} %direction_in.1), custom_call_target="tpu_custom_call" | custom-call | tf_op jit(solution)/shard_map/pallas_call | solution.py:252
  32.3 0.0 copy-start.2
  32.3 0.0 copy-start.3
  32.4 0.0 copy-done
  32.4 0.0 copy-done.1
  32.4 0.6 %copy-done.2 = f32[1,128]{1,0:T(1,128)S(1)} copy-done((f32[1,128]{1,0:T(1,128)S(1)}, f32[1,128]{1,0:T(1,128)}, u32[]{:S(2)}) %copy-start.2) | copy-done | bytes 536
  32.9 0.0 copy-done.3
  33.0 1.7 %multiply_add_fusion = (f32[256,128]{1,0:T(8,128)}, f32[256,128]{1,0:T(8,128)}, f32[256,128]{1,0:T(8,128)}) fusion(f32[256,128]{1,0:T(8,128)S(1)} %copy-done, f32[128]{0:T(128)S(1)} %bitcast.9, f32[256,128]{1,0:T(8,128)S(1)} %copy-done.1, f32[256,128]{1,0:T(8,128)} %get-tuple-element.7, f32[128]{0:T(128)S(1)} %bitcast.8, f32[256,128]{1,0:T(8,128)} %param.9), kind=kLoop, calls=%fused_computation | loop fusion | flops 196608 | bytes 918528 | tf_op jit(solution)/shard_map/add | solution.py:289
Async XLA Ops:
  1.3 31.1 %copy-start = (f32[256,128]{1,0:T(8,128)S(1)}, f32[256,128]{1,0:T(8,128)}, u32[]{:S(2)}) copy-start(f32[256,128]{1,0:T(8,128)} %direction_in.1) | copy-start | bytes 393220
  1.3 31.1 %copy-start.1 = (f32[256,128]{1,0:T(8,128)S(1)}, f32[256,128]{1,0:T(8,128)}, u32[]{:S(2)}) copy-start(f32[256,128]{1,0:T(8,128)} %residual_in.1) | copy-start | bytes 393220
  32.3 0.6 %copy-start.2 = (f32[1,128]{1,0:T(1,128)S(1)}, f32[1,128]{1,0:T(1,128)}, u32[]{:S(2)}) copy-start(f32[1,128]{1,0:T(1,128)} %get-tuple-element.6) | copy-start | bytes 1540
  32.3 0.6 %copy-start.3 = (f32[1,128]{1,0:T(1,128)S(1)}, f32[1,128]{1,0:T(1,128)}, u32[]{:S(2)}) copy-start(f32[1,128]{1,0:T(1,128)} %get-tuple-element.8) | copy-start | bytes 1540
where the time goes:
time: 34.9 us; the launch traced here: 34.7 us
  Pallas kernels  31 us (89%)
  other arithmetic  1.73 us (5%)
  between operations  1.33 us (4%)
  local copies, waits for them, and re-layouts  0.62 us (2%)
    pallas_call x1, Pallas kernels, on_device(): pl.pallas_call(functools.partial(kernel, nb, nw), out_shape=(jax.ShapeDty...  31 us
    add x1, other arithmetic, on_device(): new_direction = new_residual + ratio * direction  1.73 us

commit v1 on v0

--- a/solution.py
+++ b/solution.py
@@ -32,8 +32,8 @@
     return (poly * jnp.exp2(-root)).astype(jnp.bfloat16)
 
 
-def kernel(nb, nw, points_in, inv_in, noise_in, residual_in, direction_in, image_out, step_out, ratio_out,
-           points, inv_length, noise_var, residual, direction, image, io, feat, feat_z, rows_x, kmat, low_dir, part, part_in, stat, stat_z, stat_b, stat_o,
+def kernel(nb, nw, points_in, inv_in, noise_in, residual_in, direction_in, solution_in, solution_out, residual_out, direction_out,
+           points, inv_length, noise_var, residual, direction, old_solution, io, feat, feat_z, rows_x, kmat, low_dir, part, part_in, stat, stat_z, stat_b, stat_o,
            fs, fr, fzs, fzr, ps, pr, qs, qr, zs, zr, bs, br):
     b = lax.axis_index("blk")
     w = lax.axis_index("wide")
@@ -70,7 +70,7 @@
         pltpu.make_async_copy(src, dst, io.at[k])
         for k, (src, dst) in enumerate(
             ((points_in, points), (inv_in, inv_length), (direction_in, direction),
-             (noise_in, noise_var), (residual_in, residual))
+             (residual_in, residual), (solution_in, old_solution))
         )
     ]
     for load in loads:
@@ -205,13 +205,10 @@
         q = near(nw - k)
         part[q] = partial(q).astype(jnp.bfloat16)
         go(copy(part.at[q], part_in.at[nw - q], qs.at[q], qr.at[nw - q], along(q)))
-    total = partial(0) + noise_var[...] * direction[...]
+    total = partial(0) + noise_in[0, 0] * direction[...]
     for q in range(1, nw):
         copy(part.at[q], part_in.at[q], qs.at[q], qr.at[q], along(q)).wait_recv()
         total = total + part_in[q].astype(jnp.float32)
-    image[...] = total
-    store = pltpu.make_async_copy(image, image_out, io.at[5])
-    store.start()
 
     def column_sum(x):
         return jnp.sum(x, axis=0, keepdims=True)
@@ -235,11 +232,23 @@
         sums = sums + stat_b[slot]
     old_norm, step = sums[0:1], sums[0:1] / sums[1:2]
     new_norm = old_norm - 2.0 * step * sums[2:3] + step * step * sums[3:4]
-    step_out[...] = step
-    ratio_out[...] = new_norm / old_norm
-    store.wait()
+    new_residual = res - step * total
+    residual_out[...] = new_residual
+    solution_out[...] = old_solution[...] + step * direc
+    direction_out[...] = new_residual + new_norm / old_norm * direc
     for c in sends:
         c.wait_send()
+
+
+def write_out(a, b, c, a_out, b_out, c_out, sems):
+    copies = [
+        pltpu.make_async_copy(src, dst, sems.at[k])
+        for k, (src, dst) in enumerate(((a, a_out), (b, b_out), (c, c_out)))
+    ]
+    for copy in copies:
+        copy.start()
+    for copy in copies:
+        copy.wait()
 
 
 def on_device(nb, nw, points, inv_length, noise_var, solution, residual, direction):
@@ -249,15 +258,11 @@
     hbm = pl.BlockSpec(memory_space=pl.ANY)
     dma = pltpu.SemaphoreType.DMA
     depth = 3 * features + 2 * TAIL
-    image, step_length, ratio = pl.pallas_call(
+    news = pl.pallas_call(
         functools.partial(kernel, nb, nw),
-        out_shape=(
-            jax.ShapeDtypeStruct((piece, rhs), jnp.float32),
-            jax.ShapeDtypeStruct((1, rhs), jnp.float32),
-            jax.ShapeDtypeStruct((1, rhs), jnp.float32),
-        ),
-        in_specs=[hbm] * 5,
-        out_specs=(hbm, vmem, vmem),
+        out_shape=(pltpu.VMEM((piece, rhs), jnp.float32),) * 3,
+        in_specs=[hbm, hbm, pl.BlockSpec(memory_space=pltpu.SMEM), hbm, hbm, hbm],
+        out_specs=(vmem,) * 3,
         scratch_shapes=[
             pltpu.VMEM((features, piece), points.dtype),
             pltpu.VMEM((1, features), jnp.float32),
@@ -283,11 +288,14 @@
         compiler_params=pltpu.CompilerParams(
             collective_id=0, has_side_effects=True, vmem_limit_bytes=60 * 1024 * 1024
         ),
-    )(points.T, inv_length.reshape(1, features), noise_var.reshape(1, 1), residual, direction)
-    new_residual = residual - step_length * image
-    new_solution = solution + step_length * direction
-    new_direction = new_residual + ratio * direction
-    return (new_solution, new_residual, new_direction)
+    )(points.T, inv_length.reshape(1, features), noise_var.reshape(1, 1), residual, direction, solution)
+    return pl.pallas_call(
+        write_out,
+        out_shape=(jax.ShapeDtypeStruct((piece, rhs), jnp.float32),) * 3,
+        in_specs=[vmem] * 3,
+        out_specs=(hbm,) * 3,
+        scratch_shapes=[dma((3,))],
+    )(*(pltpu.with_memory_space_constraint(x, pltpu.VMEM) for x in news))
 
 
 def solution(mesh):

time: 34.9 us -> 32.8 us (0.940)
  other arithmetic: 1.73 us -> 0 us
  local copies, waits for them, and re-layouts: 0.62 us -> 0 us
    add x1 -> x0, other arithmetic: 1.73 us -> none  [on_device(): new_direction = new_residual + ratio * direction]
    unnamed x8 -> x0, local copies, waits for them, and re-layouts: 0.62 us -> none
    pallas_call x1 -> x2, Pallas kernels: 31 us -> 31.3 us  [the longest x1 30.5 us: on_device(): pl.pallas_call(functools.partial(kernel, nb, nw), out_shape=(pltpu.VMEM((...]
where the time goes in v1:
time: 32.8 us; the launch traced here: 32.6 us
  Pallas kernels  31.3 us (95%)
  between operations  1.28 us (4%)
    pallas_call x1, Pallas kernels, on_device(): pl.pallas_call(functools.partial(kernel, nb, nw), out_shape=(pltpu.VMEM((...  30.5 us
    pallas_call x1, Pallas kernels, on_device(): pl.pallas_call(write_out, out_shape=(jax.ShapeDtypeStruct((piece, rhs), j...  0.77 us

profile of v1, /device:TPU:0, one launch (start us, length us, event | category | flops | bytes accessed | tf_op | source)
XLA Modules:
  0.0 32.6 jit_solution(6998750237096889355)
XLA Ops:
  1.3 30.5 %shard_map.85 = (f32[256,128]{1,0:T(8,128)S(1)}, f32[256,128]{1,0:T(8,128)S(1)}, f32[256,128]{1,0:T(8,128)S(1)}) custom-call(bf16[32,256]{1,0:T(8,128)(2,1)} %bitcast.4, f32[1,32]{1,0:T(1,128)} %bitcast.5, f32[1,1]{1,0:T(1,128)} %bitcast.3.noise_in, f32[256,128]{1,0:T(8,128)} %residual_in.1, f32[256,128]{1,0:T(8,128)} %direction_in.1, f32[256,128]{1,0:T(8,128)} %solution_in.1), custom_call_target="tpu_custom_call" | custom-call | tf_op jit(solution)/shard_map/pallas_call | solution.py:261
  31.8 0.8 %shard_map.86 = (f32[256,128]{1,0:T(8,128)}, f32[256,128]{1,0:T(8,128)}, f32[256,128]{1,0:T(8,128)}) custom-call(f32[256,128]{1,0:T(8,128)S(1)} %get-tuple-element.6.a, f32[256,128]{1,0:T(8,128)S(1)} %get-tuple-element.7.b, f32[256,128]{1,0:T(8,128)S(1)} %get-tuple-element.8.c), custom_call_target="tpu_custom_call" | custom-call | tf_op jit(solution)/shard_map/pallas_call | solution.py:292

commit v2 on v1

--- a/solution.py
+++ b/solution.py
@@ -33,6 +33,210 @@
 
 
 def kernel(nb, nw, points_in, inv_in, noise_in, residual_in, direction_in, solution_in, solution_out, residual_out, direction_out,
+           points, inv_length, residual, direction, old_solution, io, feat, feat_z, rows_x, kmat, low_dir, acc, part, part_in, stat, stat_in,
+           fs, fr, fzs, fzr, ps, pr, qs, qr, ss, sr):
+    b = lax.axis_index("blk")
+    w = lax.axis_index("wide")
+    chips = nb // 2
+    chip, core = b // 2, b % 2
+    features, piece = points.shape
+
+    def other_chip(k):
+        at, bit = chip, 1
+        while bit < chips:
+            if k & bit:
+                at = at + bit - 2 * bit * lax.rem(lax.div(chip, bit), 2)
+            bit *= 2
+        return at
+
+    def same_core(k):
+        return (other_chip(k) * 2 + core, w)
+
+    sibling = (chip * 2 + 1 - core, w)
+
+    def along(q):
+        return (b, lax.rem(w + q, nw))
+
+    def at_least(limit):
+        return lax.div(w + nw - limit, nw)
+
+    upper = lax.div(2 * w, nw)
+
+    def far_first(k):
+        low = nw - 1 - k - at_least(nw - 1 - k)
+        high = k + 1 - at_least(k + 1)
+        return lax.rem(low + upper * (high - low) - w + nw, nw)
+
+    z_far = [far_first(k) for k in range(nw - 1)]
+    chips_far = sorted(range(1, chips), key=lambda k: -bin(k).count("1"))
+    chips_near = chips_far[::-1]
+
+    barrier = pltpu.get_barrier_semaphore()
+    for k in range(1, chips):
+        pl.semaphore_signal(barrier, inc=1, device_id=same_core(k), device_id_type=MESH)
+    pl.semaphore_signal(barrier, inc=1, device_id=sibling, device_id_type=MESH)
+    for q in range(1, nw):
+        pl.semaphore_signal(barrier, inc=1, device_id=along(q), device_id_type=MESH)
+
+    def copy(src, dst, send, recv, to):
+        return pltpu.make_async_remote_copy(
+            src_ref=src, dst_ref=dst, send_sem=send, recv_sem=recv, device_id=to, device_id_type=MESH
+        )
+
+    loads = [
+        pltpu.make_async_copy(src, dst, io.at[k])
+        for k, (src, dst) in enumerate(
+            ((points_in, points), (inv_in, inv_length), (direction_in, direction),
+             (residual_in, residual), (solution_in, old_solution))
+        )
+    ]
+    for load in loads:
+        load.start()
+    for load in loads[:2]:
+        load.wait()
+
+    inv_row = jnp.concatenate(
+        [inv_length[...], jnp.zeros((1, 128 - features), jnp.float32)], axis=1)
+    inv_column = jnp.broadcast_to(inv_row, (8, 128)).T[:features, 0:1]
+    x_t = rounded(points[...].astype(jnp.float32) * inv_column)
+    s1, s2, s3 = three_parts(SCALE * jnp.sum(x_t * x_t, axis=0, keepdims=True))
+    row = lax.broadcasted_iota(jnp.int32, (TAIL, piece), 0)
+    tail = jnp.where((row >= 3) & (row <= 10), 1.0, 0.0)
+    tail = jnp.where((row >= 6) & (row <= 7), 0.0, tail)
+    for at, value in ((0, s1), (1, s2), (2, s3), (11, s1), (12, s2), (13, s3)):
+        tail = jnp.where(row == at, value, tail)
+    feat[0] = jnp.concatenate([x_t, tail], axis=0).astype(jnp.bfloat16)
+    loads[2].wait()
+    low_dir[0:piece] = direction[...].astype(jnp.bfloat16)
+    pl.semaphore_wait(barrier, chips + nw - 1)
+
+    sends = []
+
+    def go(c):
+        c.start()
+        sends.append(c)
+        return c
+
+    def feat_copy(src_slot, dst_slot, to):
+        return copy(feat.at[src_slot], feat.at[dst_slot], fs.at[dst_slot], fr.at[dst_slot], to)
+
+    def dir_copy(src_slot, dst_slot, to):
+        return copy(low_dir.at[pl.ds(src_slot * piece, piece)], low_dir.at[pl.ds(dst_slot * piece, piece)],
+                    ps.at[dst_slot], pr.at[dst_slot], to)
+
+    for q in z_far:
+        go(copy(feat.at[0], feat_z.at[nw - q], fzs.at[q], fzr.at[nw - q], along(q)))
+    for k in chips_far:
+        go(feat_copy(0, k, same_core(k)))
+    go(feat_copy(0, chips, sibling))
+    for k in chips_far:
+        go(dir_copy(0, k, same_core(k)))
+    go(dir_copy(0, chips, sibling))
+    for load in loads[3:]:
+        load.wait()
+
+    def feat_arrived(slot):
+        feat_copy(slot, slot, sibling).wait_recv()
+
+    def dir_arrived(slot):
+        dir_copy(slot, slot, sibling).wait_recv()
+
+    def relay_feat(k):
+        feat_arrived(k)
+        go(feat_copy(k, chips + k, sibling))
+
+    def relay_dir(k):
+        dir_arrived(k)
+        go(dir_copy(k, chips + k, sibling))
+
+    def as_rows(block):
+        block = block.astype(jnp.float32)
+        x = block[:features]
+        h, m, l = three_parts(SCALE * x)
+        lanes = jnp.concatenate(
+            [-2.0 * h, -2.0 * m, -2.0 * l, block[features + 8 :],
+             jnp.zeros((TAIL + 8, piece), jnp.float32)], axis=0)
+        return lanes.T.astype(jnp.bfloat16)
+
+    depth = rows_x.shape[1]
+
+    def tiles(rows, slot):
+        block = feat[slot]
+        cols = jnp.concatenate(
+            [block[:features]] * 3 + [block[features:],
+             jnp.zeros((depth - 3 * features - TAIL, piece), jnp.bfloat16)], axis=0)
+        for j in rows:
+            dist = jnp.dot(rows_x[j * piece : (j + 1) * piece, :], cols, preferred_element_type=jnp.float32)
+            kmat[j * piece : (j + 1) * piece, slot * piece : (slot + 1) * piece] = matern(dist)
+
+    rows_x[0:piece] = as_rows(feat[0])
+    tiles([0], 0)
+    feat_arrived(chips)
+    tiles([0], chips)
+    for j in range(1, nw):
+        q = z_far[nw - 1 - j]
+        copy(feat_z.at[q], feat_z.at[q], fzs.at[q], fzr.at[q], along(q)).wait_recv()
+        rows_x[j * piece : (j + 1) * piece] = as_rows(feat_z[q])
+        tiles([j], 0)
+        tiles([j], chips)
+    every = range(nw)
+    for at, k in enumerate(chips_near):
+        relay_feat(k)
+        if at:
+            tiles(every, chips_near[at - 1])
+    tiles(every, chips_near[-1])
+    for k in chips_near:
+        feat_arrived(chips + k)
+        tiles(every, chips + k)
+        relay_dir(k)
+
+    half = chips * piece
+
+    def product(j, side):
+        return jnp.dot(kmat[j * piece : (j + 1) * piece, side * half : (side + 1) * half],
+                       low_dir[side * half : (side + 1) * half], preferred_element_type=jnp.float32)
+
+    for j in every:
+        acc[j] = product(j, 0)
+    for k in range(chips):
+        dir_arrived(chips + k)
+    for k in range(nw - 1):
+        j, q = nw - 1 - k, z_far[k]
+        part[j] = (acc[j] + product(j, 1)).astype(jnp.bfloat16)
+        go(copy(part.at[j], part_in.at[nw - q], qs.at[j], qr.at[nw - q], along(q)))
+    res, direc = residual[...], direction[...]
+    total = acc[0] + product(0, 1) + noise_in[0, 0] * direc
+    for q in range(1, nw):
+        copy(part_in.at[q], part_in.at[q], qs.at[q], qr.at[q], along(q)).wait_recv()
+        total = total + part_in[q].astype(jnp.float32)
+
+    for k, value in enumerate((res * res, direc * total, res * total, total * total)):
+        stat[k : k + 1] = jnp.sum(value, axis=0, keepdims=True)
+    for r, q in enumerate(z_far + [0]):
+        for k in chips_far + [0]:
+            for c in range(2):
+                if r == nw - 1 and k == 0 and c == 0:
+                    continue
+                to = (other_chip(k) * 2 + (core if c == 0 else 1 - core), lax.rem(w + q, nw))
+                slot = (lax.rem(nw - q, nw) * 2 + c) * chips + k
+                go(copy(stat, stat_in.at[slot], ss.at[0], sr.at[0], to))
+    others = stat_in.at[pl.ds(1, nb * nw - 1)]
+    copy(others, others, ss.at[0], sr.at[0], sibling).wait_recv()
+    sums = stat[...]
+    for slot in range(1, nb * nw):
+        sums = sums + stat_in[slot]
+    old_norm, step = sums[0:1], sums[0:1] / sums[1:2]
+    new_norm = old_norm - 2.0 * step * sums[2:3] + step * step * sums[3:4]
+    new_residual = res - step * total
+    residual_out[...] = new_residual
+    solution_out[...] = old_solution[...] + step * direc
+    direction_out[...] = new_residual + new_norm / old_norm * direc
+    for c in sends[: len(sends) - (nb * nw - 1)]:
+        c.wait_send()
+    copy(others, others, ss.at[0], sr.at[0], sibling).wait_send()
+
+
+def long_kernel(nb, nw, points_in, inv_in, noise_in, residual_in, direction_in, solution_in, solution_out, residual_out, direction_out,
            points, inv_length, noise_var, residual, direction, old_solution, io, feat, feat_z, rows_x, kmat, low_dir, part, part_in, stat, stat_z, stat_b, stat_o,
            fs, fr, fzs, fzr, ps, pr, qs, qr, zs, zr, bs, br):
     b = lax.axis_index("blk")
@@ -258,33 +462,40 @@
     hbm = pl.BlockSpec(memory_space=pl.ANY)
     dma = pltpu.SemaphoreType.DMA
     depth = 3 * features + 2 * TAIL
-    news = pl.pallas_call(
-        functools.partial(kernel, nb, nw),
-        out_shape=(pltpu.VMEM((piece, rhs), jnp.float32),) * 3,
-        in_specs=[hbm, hbm, pl.BlockSpec(memory_space=pltpu.SMEM), hbm, hbm, hbm],
-        out_specs=(vmem,) * 3,
-        scratch_shapes=[
-            pltpu.VMEM((features, piece), points.dtype),
-            pltpu.VMEM((1, features), jnp.float32),
-            pltpu.VMEM((1, 1), jnp.float32),
-            pltpu.VMEM((piece, rhs), jnp.float32),
-            pltpu.VMEM((piece, rhs), jnp.float32),
-            pltpu.VMEM((piece, rhs), jnp.float32),
-            dma((6,)),
-            pltpu.VMEM((nb, features + TAIL, piece), jnp.bfloat16),
-            pltpu.VMEM((nw, features + TAIL, piece), jnp.bfloat16),
-            pltpu.VMEM((nw * piece, depth), jnp.bfloat16),
-            pltpu.VMEM((nw * piece, nb * piece), jnp.bfloat16),
-            pltpu.VMEM((nb * piece, rhs), jnp.bfloat16),
-            pltpu.VMEM((nw, piece, rhs), jnp.bfloat16),
-            pltpu.VMEM((nw, piece, rhs), jnp.bfloat16),
+    common = [
+        pltpu.VMEM((features, piece), points.dtype),
+        pltpu.VMEM((1, features), jnp.float32),
+    ]
+    wide = [
+        dma((6,)),
+        pltpu.VMEM((nb, features + TAIL, piece), jnp.bfloat16),
+        pltpu.VMEM((nw, features + TAIL, piece), jnp.bfloat16),
+        pltpu.VMEM((nw * piece, depth), jnp.bfloat16),
+        pltpu.VMEM((nw * piece, nb * piece), jnp.bfloat16),
+        pltpu.VMEM((nb * piece, rhs), jnp.bfloat16),
+    ]
+    vectors = [pltpu.VMEM((piece, rhs), jnp.float32)] * 3
+    parts = [pltpu.VMEM((nw, piece, rhs), jnp.bfloat16)] * 2
+    sems = [dma((nb,)), dma((nb,)), dma((nw,)), dma((nw,)), dma((nb,)), dma((nb,)), dma((nw,)), dma((nw,))]
+    if nw <= 4:
+        body = kernel
+        scratch = common + vectors + wide + [pltpu.VMEM((nw, piece, rhs), jnp.float32)] + parts + [
+            pltpu.VMEM((4, rhs), jnp.float32), pltpu.VMEM((nw * nb, 4, rhs), jnp.float32),
+        ] + sems + [dma((1,)), dma((1,))]
+    else:
+        body = long_kernel
+        scratch = common + [pltpu.VMEM((1, 1), jnp.float32)] + vectors + wide + parts + [
             pltpu.VMEM((8, rhs), jnp.float32),
             pltpu.VMEM((nw, 8, rhs), jnp.float32),
             pltpu.VMEM((nb, 8, rhs), jnp.float32),
             pltpu.VMEM((8, rhs), jnp.float32),
-            dma((nb,)), dma((nb,)), dma((nw,)), dma((nw,)), dma((nb,)), dma((nb,)),
-            dma((nw,)), dma((nw,)), dma((nw,)), dma((nw,)), dma((nb,)), dma((nb,)),
-        ],
+        ] + sems + [dma((nw,)), dma((nw,)), dma((nb,)), dma((nb,))]
+    news = pl.pallas_call(
+        functools.partial(body, nb, nw),
+        out_shape=(pltpu.VMEM((piece, rhs), jnp.float32),) * 3,
+        in_specs=[hbm, hbm, pl.BlockSpec(memory_space=pltpu.SMEM), hbm, hbm, hbm],
+        out_specs=(vmem,) * 3,
+        scratch_shapes=scratch,
         compiler_params=pltpu.CompilerParams(
             collective_id=0, has_side_effects=True, vmem_limit_bytes=60 * 1024 * 1024
         ),

time: 32.8 us -> 30 us (0.915)
  Pallas kernels: 31.3 us -> 28.4 us
    pallas_call x1, Pallas kernels: 30.5 us -> 27.6 us  [on_device(): pl.pallas_call(functools.partial(body, nb, nw), out_shape=(pltpu.VMEM((pi...]
where the time goes in v2:
time: 30 us; the launch traced here: 29.7 us
  Pallas kernels  28.4 us (95%)
  between operations  1.28 us (4%)
    pallas_call x1, Pallas kernels, on_device(): pl.pallas_call(functools.partial(body, nb, nw), out_shape=(pltpu.VMEM((pi...  27.6 us
    pallas_call x1, Pallas kernels, on_device(): pl.pallas_call(write_out, out_shape=(jax.ShapeDtypeStruct((piece, rhs), j...  0.77 us

profile of v2, /device:TPU:0, one launch (start us, length us, event | category | flops | bytes accessed | tf_op | source)
XLA Modules:
  0.0 29.7 jit_solution(13966227604641899073)
XLA Ops:
  1.3 27.6 %shard_map.85 = (f32[256,128]{1,0:T(8,128)S(1)}, f32[256,128]{1,0:T(8,128)S(1)}, f32[256,128]{1,0:T(8,128)S(1)}) custom-call(bf16[32,256]{1,0:T(8,128)(2,1)} %bitcast.4, f32[1,32]{1,0:T(1,128)} %bitcast.5, f32[1,1]{1,0:T(1,128)} %bitcast.3.noise_in, f32[256,128]{1,0:T(8,128)} %residual_in.1, f32[256,128]{1,0:T(8,128)} %direction_in.1, f32[256,128]{1,0:T(8,128)} %solution_in.1), custom_call_target="tpu_custom_call" | custom-call | tf_op jit(solution)/shard_map/pallas_call | solution.py:493
  28.9 0.8 %shard_map.86 = (f32[256,128]{1,0:T(8,128)}, f32[256,128]{1,0:T(8,128)}, f32[256,128]{1,0:T(8,128)}) custom-call(f32[256,128]{1,0:T(8,128)S(1)} %get-tuple-element.6.a, f32[256,128]{1,0:T(8,128)S(1)} %get-tuple-element.7.b, f32[256,128]{1,0:T(8,128)S(1)} %get-tuple-element.8.c), custom_call_target="tpu_custom_call" | custom-call | tf_op jit(solution)/shard_map/pallas_call | solution.py:503

commit v3 on v2

--- a/solution.py
+++ b/solution.py
@@ -33,8 +33,8 @@
 
 
 def kernel(nb, nw, points_in, inv_in, noise_in, residual_in, direction_in, solution_in, solution_out, residual_out, direction_out,
-           points, inv_length, residual, direction, old_solution, io, feat, feat_z, rows_x, kmat, low_dir, acc, part, part_in, stat, stat_in,
-           fs, fr, fzs, fzr, ps, pr, qs, qr, ss, sr):
+           points, inv_length, residual, direction, old_solution, io, feat, feat_z, rows_x, cols_x, kmat, dir_a, dir_b, part_a, part_a_in, part_b, part_b_in, stat, stat_in,
+           fs, fr, fzs, fzr, as_, ar, bs, br, qs, qr, ts, tr, ss, sr):
     b = lax.axis_index("blk")
     w = lax.axis_index("wide")
     chips = nb // 2
@@ -99,15 +99,12 @@
         [inv_length[...], jnp.zeros((1, 128 - features), jnp.float32)], axis=1)
     inv_column = jnp.broadcast_to(inv_row, (8, 128)).T[:features, 0:1]
     x_t = rounded(points[...].astype(jnp.float32) * inv_column)
-    s1, s2, s3 = three_parts(SCALE * jnp.sum(x_t * x_t, axis=0, keepdims=True))
-    row = lax.broadcasted_iota(jnp.int32, (TAIL, piece), 0)
-    tail = jnp.where((row >= 3) & (row <= 10), 1.0, 0.0)
-    tail = jnp.where((row >= 6) & (row <= 7), 0.0, tail)
-    for at, value in ((0, s1), (1, s2), (2, s3), (11, s1), (12, s2), (13, s3)):
-        tail = jnp.where(row == at, value, tail)
-    feat[0] = jnp.concatenate([x_t, tail], axis=0).astype(jnp.bfloat16)
+    feat[0] = x_t.astype(jnp.bfloat16)
     loads[2].wait()
-    low_dir[0:piece] = direction[...].astype(jnp.bfloat16)
+    dir_t = direction[...].T.astype(jnp.bfloat16)
+    part = dir_t.shape[0] // 2
+    dir_a[0] = dir_t[:part]
+    dir_b[0] = dir_t[part:]
     pl.semaphore_wait(barrier, chips + nw - 1)
 
     sends = []
@@ -121,8 +118,7 @@
         return copy(feat.at[src_slot], feat.at[dst_slot], fs.at[dst_slot], fr.at[dst_slot], to)
 
     def dir_copy(src_slot, dst_slot, to):
-        return copy(low_dir.at[pl.ds(src_slot * piece, piece)], low_dir.at[pl.ds(dst_slot * piece, piece)],
-                    ps.at[dst_slot], pr.at[dst_slot], to)
+        return copy(dir_a.at[src_slot], dir_a.at[dst_slot], as_.at[dst_slot], ar.at[dst_slot], to)
 
     for q in z_far:
         go(copy(feat.at[0], feat_z.at[nw - q], fzs.at[q], fzr.at[nw - q], along(q)))
@@ -131,6 +127,8 @@
     go(feat_copy(0, chips, sibling))
     for k in chips_far:
         go(dir_copy(0, k, same_core(k)))
+    for q in z_far:
+        go(copy(dir_b.at[0], dir_b.at[nw - q], bs.at[q], br.at[nw - q], along(q)))
     go(dir_copy(0, chips, sibling))
     for load in loads[3:]:
         load.wait()
@@ -149,66 +147,119 @@
         dir_arrived(k)
         go(dir_copy(k, chips + k, sibling))
 
-    def as_rows(block):
-        block = block.astype(jnp.float32)
-        x = block[:features]
-        h, m, l = three_parts(SCALE * x)
+    depth = rows_x.shape[1]
+    ones = jnp.where(lax.broadcasted_iota(jnp.int32, (8, piece), 0) < 3, 1.0, 0.0)
+    at = lax.broadcasted_iota(jnp.int32, (8, piece), 0)
+    blank = jnp.zeros((depth - 3 * features - 16, piece), jnp.float32)
+
+    def norms(x, first):
+        result = jnp.zeros((8, piece), jnp.float32)
+        for k, value in enumerate(three_parts(SCALE * jnp.sum(x * x, axis=0, keepdims=True))):
+            result = jnp.where(at == first + k, value, result)
+        return result
+
+    def make_rows(j, block):
+        x = block.astype(jnp.float32)
         lanes = jnp.concatenate(
-            [-2.0 * h, -2.0 * m, -2.0 * l, block[features + 8 :],
-             jnp.zeros((TAIL + 8, piece), jnp.float32)], axis=0)
-        return lanes.T.astype(jnp.bfloat16)
-
-    depth = rows_x.shape[1]
-
-    def tiles(rows, slot):
+            [-2.0 * value for value in three_parts(SCALE * x)] + [ones, norms(x, 0), blank], axis=0)
+        rows_x[j * piece : (j + 1) * piece] = lanes.T.astype(jnp.bfloat16)
+
+    def make_cols(slot):
         block = feat[slot]
-        cols = jnp.concatenate(
-            [block[:features]] * 3 + [block[features:],
-             jnp.zeros((depth - 3 * features - TAIL, piece), jnp.bfloat16)], axis=0)
-        for j in rows:
-            dist = jnp.dot(rows_x[j * piece : (j + 1) * piece, :], cols, preferred_element_type=jnp.float32)
-            kmat[j * piece : (j + 1) * piece, slot * piece : (slot + 1) * piece] = matern(dist)
-
-    rows_x[0:piece] = as_rows(feat[0])
-    tiles([0], 0)
+        tail = jnp.concatenate([norms(block.astype(jnp.float32), 0), ones, blank], axis=0)
+        cols_x[slot] = jnp.concatenate([block] * 3 + [tail.astype(jnp.bfloat16)], axis=0)
+
+    def at_rows(j):
+        return slice(j * piece, (j + 1) * piece)
+
+    def tiles(rows, slots):
+        for slot in slots:
+            for j in rows:
+                dist = jnp.dot(rows_x[at_rows(j), :], cols_x[slot], preferred_element_type=jnp.float32)
+                kmat[at_rows(j), at_rows(slot)] = matern(dist)
+
+    z_near = [0] + z_far[::-1]
+
+    def next_rows(j, slots):
+        q = z_near[j]
+        copy(feat_z.at[q], feat_z.at[q], fzs.at[q], fzr.at[q], along(q)).wait_recv()
+        make_rows(j, feat_z[q])
+        tiles([j], slots)
+
+    make_rows(0, feat[0])
+    make_cols(0)
+    tiles([0], [0])
     feat_arrived(chips)
-    tiles([0], chips)
-    for j in range(1, nw):
-        q = z_far[nw - 1 - j]
-        copy(feat_z.at[q], feat_z.at[q], fzs.at[q], fzr.at[q], along(q)).wait_recv()
-        rows_x[j * piece : (j + 1) * piece] = as_rows(feat_z[q])
-        tiles([j], 0)
-        tiles([j], chips)
+    make_cols(chips)
+    tiles([0], [chips])
+    have_rows, have_cols = 1, [0, chips]
+    for step in range(max(chips, nw)):
+        if have_rows < nw:
+            next_rows(have_rows, have_cols)
+            have_rows += 1
+        new = chips_near[: -1] if step == 0 else chips_near[-1:] if step == 1 else []
+        for k in new:
+            relay_feat(k)
+        for k in new:
+            make_cols(k)
+            tiles(range(have_rows), [k])
+            have_cols.append(k)
     every = range(nw)
-    for at, k in enumerate(chips_near):
-        relay_feat(k)
-        if at:
-            tiles(every, chips_near[at - 1])
-    tiles(every, chips_near[-1])
     for k in chips_near:
         feat_arrived(chips + k)
-        tiles(every, chips + k)
+        make_cols(chips + k)
+        tiles(every, [chips + k])
         relay_dir(k)
 
-    half = chips * piece
-
-    def product(j, side):
-        return jnp.dot(kmat[j * piece : (j + 1) * piece, side * half : (side + 1) * half],
-                       low_dir[side * half : (side + 1) * half], preferred_element_type=jnp.float32)
-
-    for j in every:
-        acc[j] = product(j, 0)
+    def product_a(j):
+        total = None
+        for slot in range(nb):
+            term = lax.dot_general(kmat[at_rows(j), at_rows(slot)], dir_a[slot], (((1,), (1,)), ((), ())),
+                                   preferred_element_type=jnp.float32)
+            total = term if total is None else total + term
+        return total.T
+
+    def product_b(slot):
+        total = None
+        for j in every:
+            term = jnp.dot(dir_b[z_near[j]], kmat[at_rows(j), at_rows(slot)],
+                           preferred_element_type=jnp.float32)
+            total = term if total is None else total + term
+        return total
+
+    def send_a(j):
+        q = z_near[j]
+        part_a[j] = product_a(j).astype(jnp.bfloat16)
+        go(copy(part_a.at[j], part_a_in.at[nw - q], qs.at[j], qr.at[nw - q], along(q)))
+
+    def send_b(k, c):
+        slot = c * chips + k
+        to = (other_chip(k) * 2 + (1 - core if c else core), w)
+        part_b[slot] = product_b(slot).astype(jnp.bfloat16)
+        go(copy(part_b.at[slot], part_b_in.at[slot], ts.at[slot], tr.at[slot], to))
+
     for k in range(chips):
         dir_arrived(chips + k)
-    for k in range(nw - 1):
-        j, q = nw - 1 - k, z_far[k]
-        part[j] = (acc[j] + product(j, 1)).astype(jnp.bfloat16)
-        go(copy(part.at[j], part_in.at[nw - q], qs.at[j], qr.at[nw - q], along(q)))
+    send_a(nw - 1)
+    for q in z_near[1:]:
+        copy(dir_b.at[q], dir_b.at[q], bs.at[q], br.at[q], along(q)).wait_recv()
+    for at_k, k in enumerate(chips_far):
+        for c in range(2):
+            send_b(k, c)
+        if nw - 2 - at_k > 0:
+            send_a(nw - 2 - at_k)
+    for j in range(nw - 1 - len(chips_far) - 1, 0, -1):
+        send_a(j)
+    send_b(0, 1)
+    total_a, total_b = product_a(0), product_b(0)
+    for q in z_near[1:]:
+        copy(part_a_in.at[q], part_a_in.at[q], qs.at[0], qr.at[q], along(q)).wait_recv()
+        total_a = total_a + part_a_in[q].astype(jnp.float32)
+    for slot in range(1, nb):
+        copy(part_b_in.at[slot], part_b_in.at[slot], ts.at[0], tr.at[slot], sibling).wait_recv()
+        total_b = total_b + part_b_in[slot].astype(jnp.float32)
     res, direc = residual[...], direction[...]
-    total = acc[0] + product(0, 1) + noise_in[0, 0] * direc
-    for q in range(1, nw):
-        copy(part_in.at[q], part_in.at[q], qs.at[q], qr.at[q], along(q)).wait_recv()
-        total = total + part_in[q].astype(jnp.float32)
+    total = jnp.concatenate([total_a, total_b], axis=0).T + noise_in[0, 0] * direc
 
     for k, value in enumerate((res * res, direc * total, res * total, total * total)):
         stat[k : k + 1] = jnp.sum(value, axis=0, keepdims=True)
@@ -479,9 +530,18 @@
     sems = [dma((nb,)), dma((nb,)), dma((nw,)), dma((nw,)), dma((nb,)), dma((nb,)), dma((nw,)), dma((nw,))]
     if nw <= 4:
         body = kernel
-        scratch = common + vectors + wide + [pltpu.VMEM((nw, piece, rhs), jnp.float32)] + parts + [
+        half = rhs // 2
+        low = jnp.bfloat16
+        scratch = common + vectors + [
+            dma((6,)),
+            pltpu.VMEM((nb, features, piece), low), pltpu.VMEM((nw, features, piece), low),
+            pltpu.VMEM((nw * piece, depth), low), pltpu.VMEM((nb, depth, piece), low),
+            pltpu.VMEM((nw * piece, nb * piece), low),
+            pltpu.VMEM((nb, half, piece), low), pltpu.VMEM((nw, half, piece), low),
+            pltpu.VMEM((nw, half, piece), low), pltpu.VMEM((nw, half, piece), low),
+            pltpu.VMEM((nb, half, piece), low), pltpu.VMEM((nb, half, piece), low),
             pltpu.VMEM((4, rhs), jnp.float32), pltpu.VMEM((nw * nb, 4, rhs), jnp.float32),
-        ] + sems + [dma((1,)), dma((1,))]
+        ] + sems + [dma((nw,)), dma((nw,)), dma((nb,)), dma((nb,)), dma((1,)), dma((1,))]
     else:
         body = long_kernel
         scratch = common + [pltpu.VMEM((1, 1), jnp.float32)] + vectors + wide + parts + [

time: 30 us -> 28.3 us (0.943)
  Pallas kernels: 28.4 us -> 26.7 us
    pallas_call x1, Pallas kernels: 27.6 us -> 26 us  [on_device(): pl.pallas_call(functools.partial(body, nb, nw), out_shape=(pltpu.VMEM((pi...]
where the time goes in v3:
time: 28.3 us; the launch traced here: 28 us
  Pallas kernels  26.7 us (94%)
  between operations  1.28 us (5%)
    pallas_call x1, Pallas kernels, on_device(): pl.pallas_call(functools.partial(body, nb, nw), out_shape=(pltpu.VMEM((pi...  26 us
    pallas_call x1, Pallas kernels, on_device(): pl.pallas_call(write_out, out_shape=(jax.ShapeDtypeStruct((piece, rhs), j...  0.77 us

profile of v3, /device:TPU:0, one launch (start us, length us, event | category | flops | bytes accessed | tf_op | source)
XLA Modules:
  0.0 28.0 jit_solution(10043523535188717009)
XLA Ops:
  1.3 26.0 %shard_map.85 = (f32[256,128]{1,0:T(8,128)S(1)}, f32[256,128]{1,0:T(8,128)S(1)}, f32[256,128]{1,0:T(8,128)S(1)}) custom-call(bf16[32,256]{1,0:T(8,128)(2,1)} %bitcast.4, f32[1,32]{1,0:T(1,128)} %bitcast.5, f32[1,1]{1,0:T(1,128)} %bitcast.3.noise_in, f32[256,128]{1,0:T(8,128)} %residual_in.1, f32[256,128]{1,0:T(8,128)} %direction_in.1, f32[256,128]{1,0:T(8,128)} %solution_in.1), custom_call_target="tpu_custom_call" | custom-call | tf_op jit(solution)/shard_map/pallas_call | solution.py:553
  27.2 0.8 %shard_map.86 = (f32[256,128]{1,0:T(8,128)}, f32[256,128]{1,0:T(8,128)}, f32[256,128]{1,0:T(8,128)}) custom-call(f32[256,128]{1,0:T(8,128)S(1)} %get-tuple-element.6.a, f32[256,128]{1,0:T(8,128)S(1)} %get-tuple-element.7.b, f32[256,128]{1,0:T(8,128)S(1)} %get-tuple-element.8.c), custom_call_target="tpu_custom_call" | custom-call | tf_op jit(solution)/shard_map/pallas_call | solution.py:563

commit v4 on v3

--- a/solution.py
+++ b/solution.py
@@ -33,8 +33,8 @@
 
 
 def kernel(nb, nw, points_in, inv_in, noise_in, residual_in, direction_in, solution_in, solution_out, residual_out, direction_out,
-           points, inv_length, residual, direction, old_solution, io, feat, feat_z, rows_x, cols_x, kmat, dir_a, dir_b, part_a, part_a_in, part_b, part_b_in, stat, stat_in,
-           fs, fr, fzs, fzr, as_, ar, bs, br, qs, qr, ts, tr, ss, sr):
+           points, inv_length, direction, others, io, feat, feat_z, rows_x, cols_x, kmat, dir_a, dir_b, dir_rows, part_a, part_a_in, part_b, part_b_in, stat, stat_in,
+           sent, feat_sem, feat_z_sem, dir_sem, got):
     b = lax.axis_index("blk")
     w = lax.axis_index("wide")
     chips = nb // 2
@@ -84,10 +84,10 @@
         )
 
     loads = [
-        pltpu.make_async_copy(src, dst, io.at[k])
+        pltpu.make_async_copy(src, dst, io.at[min(k, 3)])
         for k, (src, dst) in enumerate(
             ((points_in, points), (inv_in, inv_length), (direction_in, direction),
-             (residual_in, residual), (solution_in, old_solution))
+             (residual_in, others.at[0]), (solution_in, others.at[1]))
         )
     ]
     for load in loads:
@@ -100,52 +100,47 @@
     inv_column = jnp.broadcast_to(inv_row, (8, 128)).T[:features, 0:1]
     x_t = rounded(points[...].astype(jnp.float32) * inv_column)
     feat[0] = x_t.astype(jnp.bfloat16)
+    pl.semaphore_wait(barrier, chips + nw - 1)
+
+    FEAT, FEAT_Z, DIR, DIR_Z, PART, PART_Z, STAT = range(7)
+
+    def feat_copy(src_slot, dst_slot, to):
+        return copy(feat.at[src_slot], feat.at[dst_slot], sent.at[FEAT], feat_sem.at[dst_slot - 1], to)
+
+    def dir_copy(src_slot, dst_slot, to):
+        return copy(dir_a.at[src_slot], dir_a.at[dst_slot], sent.at[DIR], dir_sem.at[min(dst_slot, chips) - 1], to)
+
+    def feat_z_copy(src, slot, q):
+        return copy(src, feat_z.at[slot], sent.at[FEAT_Z], feat_z_sem.at[slot - 1], along(q))
+
+    for q in z_far:
+        feat_z_copy(feat.at[0], nw - q, q).start()
+    for k in chips_far:
+        feat_copy(0, k, same_core(k)).start()
+    feat_copy(0, chips, sibling).start()
     loads[2].wait()
     dir_t = direction[...].T.astype(jnp.bfloat16)
     part = dir_t.shape[0] // 2
     dir_a[0] = dir_t[:part]
     dir_b[0] = dir_t[part:]
-    pl.semaphore_wait(barrier, chips + nw - 1)
-
-    sends = []
-
-    def go(c):
-        c.start()
-        sends.append(c)
-        return c
-
-    def feat_copy(src_slot, dst_slot, to):
-        return copy(feat.at[src_slot], feat.at[dst_slot], fs.at[dst_slot], fr.at[dst_slot], to)
-
-    def dir_copy(src_slot, dst_slot, to):
-        return copy(dir_a.at[src_slot], dir_a.at[dst_slot], as_.at[dst_slot], ar.at[dst_slot], to)
-
-    for q in z_far:
-        go(copy(feat.at[0], feat_z.at[nw - q], fzs.at[q], fzr.at[nw - q], along(q)))
     for k in chips_far:
-        go(feat_copy(0, k, same_core(k)))
-    go(feat_copy(0, chips, sibling))
-    for k in chips_far:
-        go(dir_copy(0, k, same_core(k)))
-    for q in z_far:
-        go(copy(dir_b.at[0], dir_b.at[nw - q], bs.at[q], br.at[nw - q], along(q)))
-    go(dir_copy(0, chips, sibling))
-    for load in loads[3:]:
-        load.wait()
+        dir_copy(0, k, same_core(k)).start()
+    dir_copy(0, chips, sibling).start()
+    dir_rows[0:piece] = direction[...][:, :part].astype(jnp.bfloat16)
 
     def feat_arrived(slot):
         feat_copy(slot, slot, sibling).wait_recv()
 
-    def dir_arrived(slot):
-        dir_copy(slot, slot, sibling).wait_recv()
-
     def relay_feat(k):
         feat_arrived(k)
-        go(feat_copy(k, chips + k, sibling))
+        feat_copy(k, chips + k, sibling).start()
+
+    def turn(slot):
+        dir_rows[at_rows(slot), :] = dir_a[slot].astype(jnp.float32).T.astype(jnp.bfloat16)
 
     def relay_dir(k):
-        dir_arrived(k)
-        go(dir_copy(k, chips + k, sibling))
+        dir_copy(k, k, sibling).wait_recv()
+        dir_copy(k, chips + k, sibling).start()
 
     depth = rows_x.shape[1]
     ones = jnp.where(lax.broadcasted_iota(jnp.int32, (8, piece), 0) < 3, 1.0, 0.0)
@@ -180,44 +175,58 @@
 
     z_near = [0] + z_far[::-1]
 
-    def next_rows(j, slots):
-        q = z_near[j]
-        copy(feat_z.at[q], feat_z.at[q], fzs.at[q], fzr.at[q], along(q)).wait_recv()
-        make_rows(j, feat_z[q])
-        tiles([j], slots)
-
-    make_rows(0, feat[0])
-    make_cols(0)
-    tiles([0], [0])
-    feat_arrived(chips)
-    make_cols(chips)
-    tiles([0], [chips])
-    have_rows, have_cols = 1, [0, chips]
-    for step in range(max(chips, nw)):
-        if have_rows < nw:
-            next_rows(have_rows, have_cols)
-            have_rows += 1
-        new = chips_near[: -1] if step == 0 else chips_near[-1:] if step == 1 else []
-        for k in new:
-            relay_feat(k)
-        for k in new:
-            make_cols(k)
-            tiles(range(have_rows), [k])
-            have_cols.append(k)
+    have_rows, have_cols = [], []
+
+    def add_rows(j):
+        if j:
+            q = z_near[j]
+            feat_z_copy(feat_z.at[q], q, q).wait_recv()
+            make_rows(j, feat_z[q])
+        else:
+            make_rows(0, feat[0])
+        tiles([j], have_cols)
+        have_rows.append(j)
+
+    def add_cols(slot):
+        if slot >= chips:
+            feat_arrived(slot)
+        make_cols(slot)
+        tiles(have_rows, [slot])
+        have_cols.append(slot)
+
     every = range(nw)
-    for k in chips_near:
-        feat_arrived(chips + k)
-        make_cols(chips + k)
-        tiles(every, [chips + k])
+    near, last = chips_near[:-1], chips_near[-1:]
+    add_rows(0)
+    add_cols(0)
+    add_cols(chips)
+    for q in z_far:
+        copy(dir_b.at[0], dir_b.at[nw - q], sent.at[DIR_Z], got.at[DIR_Z], along(q)).start()
+    for k in near:
+        relay_feat(k)
+    for k in near:
+        add_cols(k)
+    if nw > 1:
+        add_rows(1)
+    for k in last:
+        relay_feat(k)
+        add_cols(k)
+    for k in near:
+        add_cols(chips + k)
+    for j in range(2, nw - 1):
+        add_rows(j)
+    for k in near:
         relay_dir(k)
+    for j in range(max(2, nw - 1), nw):
+        add_rows(j)
+    for k in last:
+        relay_dir(k)
+    for k in range(1, chips):
+        turn(k)
+    for k in last:
+        add_cols(chips + k)
 
     def product_a(j):
-        total = None
-        for slot in range(nb):
-            term = lax.dot_general(kmat[at_rows(j), at_rows(slot)], dir_a[slot], (((1,), (1,)), ((), ())),
-                                   preferred_element_type=jnp.float32)
-            total = term if total is None else total + term
-        return total.T
+        return jnp.dot(kmat[at_rows(j), :], dir_rows[...], preferred_element_type=jnp.float32).T
 
     def product_b(slot):
         total = None
@@ -230,19 +239,23 @@
     def send_a(j):
         q = z_near[j]
         part_a[j] = product_a(j).astype(jnp.bfloat16)
-        go(copy(part_a.at[j], part_a_in.at[nw - q], qs.at[j], qr.at[nw - q], along(q)))
+        copy(part_a.at[j], part_a_in.at[nw - q], sent.at[PART_Z], got.at[PART_Z], along(q)).start()
 
     def send_b(k, c):
         slot = c * chips + k
         to = (other_chip(k) * 2 + (1 - core if c else core), w)
         part_b[slot] = product_b(slot).astype(jnp.bfloat16)
-        go(copy(part_b.at[slot], part_b_in.at[slot], ts.at[slot], tr.at[slot], to))
-
+        copy(part_b.at[slot], part_b_in.at[slot], sent.at[PART], got.at[PART], to).start()
+
+    def all_of(ref, kind, recv):
+        return copy(ref, ref, sent.at[kind], recv, sibling)
+
+    relayed, z_dirs = dir_a.at[pl.ds(chips, chips)], dir_b.at[pl.ds(1, nw - 1)]
+    all_of(relayed, DIR, dir_sem.at[chips - 1]).wait_recv()
     for k in range(chips):
-        dir_arrived(chips + k)
+        turn(chips + k)
     send_a(nw - 1)
-    for q in z_near[1:]:
-        copy(dir_b.at[q], dir_b.at[q], bs.at[q], br.at[q], along(q)).wait_recv()
+    all_of(z_dirs, DIR_Z, got.at[DIR_Z]).wait_recv()
     for at_k, k in enumerate(chips_far):
         for c in range(2):
             send_b(k, c)
@@ -252,13 +265,16 @@
         send_a(j)
     send_b(0, 1)
     total_a, total_b = product_a(0), product_b(0)
-    for q in z_near[1:]:
-        copy(part_a_in.at[q], part_a_in.at[q], qs.at[0], qr.at[q], along(q)).wait_recv()
+    parts_z, parts_b = part_a_in.at[pl.ds(1, nw - 1)], part_b_in.at[pl.ds(1, nb - 1)]
+    all_of(parts_z, PART_Z, got.at[PART_Z]).wait_recv()
+    for q in range(1, nw):
         total_a = total_a + part_a_in[q].astype(jnp.float32)
+    all_of(parts_b, PART, got.at[PART]).wait_recv()
     for slot in range(1, nb):
-        copy(part_b_in.at[slot], part_b_in.at[slot], ts.at[0], tr.at[slot], sibling).wait_recv()
         total_b = total_b + part_b_in[slot].astype(jnp.float32)
-    res, direc = residual[...], direction[...]
+    make_vectors = pltpu.make_async_copy(others, others, io.at[3])
+    make_vectors.wait()
+    res, direc = others[0], direction[...]
     total = jnp.concatenate([total_a, total_b], axis=0).T + noise_in[0, 0] * direc
 
     for k, value in enumerate((res * res, direc * total, res * total, total * total)):
@@ -270,9 +286,9 @@
                     continue
                 to = (other_chip(k) * 2 + (core if c == 0 else 1 - core), lax.rem(w + q, nw))
                 slot = (lax.rem(nw - q, nw) * 2 + c) * chips + k
-                go(copy(stat, stat_in.at[slot], ss.at[0], sr.at[0], to))
-    others = stat_in.at[pl.ds(1, nb * nw - 1)]
-    copy(others, others, ss.at[0], sr.at[0], sibling).wait_recv()
+                copy(stat, stat_in.at[slot], sent.at[STAT], got.at[STAT], to).start()
+    stats = stat_in.at[pl.ds(1, nb * nw - 1)]
+    all_of(stats, STAT, got.at[STAT]).wait_recv()
     sums = stat[...]
     for slot in range(1, nb * nw):
         sums = sums + stat_in[slot]
@@ -280,11 +296,11 @@
     new_norm = old_norm - 2.0 * step * sums[2:3] + step * step * sums[3:4]
     new_residual = res - step * total
     residual_out[...] = new_residual
-    solution_out[...] = old_solution[...] + step * direc
+    solution_out[...] = others[1] + step * direc
     direction_out[...] = new_residual + new_norm / old_norm * direc
-    for c in sends[: len(sends) - (nb * nw - 1)]:
-        c.wait_send()
-    copy(others, others, ss.at[0], sr.at[0], sibling).wait_send()
+    for ref, kind in ((feat.at[pl.ds(1, nb - 1)], FEAT), (feat_z.at[pl.ds(1, nw - 1)], FEAT_Z), (dir_a.at[pl.ds(1, nb - 1)], DIR),
+                      (z_dirs, DIR_Z), (parts_b, PART), (parts_z, PART_Z), (stats, STAT)):
+        all_of(ref, kind, got.at[kind]).wait_send()
 
 
 def long_kernel(nb, nw, points_in, inv_in, noise_in, residual_in, direction_in, solution_in, solution_out, residual_out, direction_out,
@@ -532,16 +548,18 @@
         body = kernel
         half = rhs // 2
         low = jnp.bfloat16
-        scratch = common + vectors + [
-            dma((6,)),
+        scratch = common + [
+            pltpu.VMEM((piece, rhs), jnp.float32), pltpu.VMEM((2, piece, rhs), jnp.float32), dma((4,)),
             pltpu.VMEM((nb, features, piece), low), pltpu.VMEM((nw, features, piece), low),
             pltpu.VMEM((nw * piece, depth), low), pltpu.VMEM((nb, depth, piece), low),
             pltpu.VMEM((nw * piece, nb * piece), low),
             pltpu.VMEM((nb, half, piece), low), pltpu.VMEM((nw, half, piece), low),
+            pltpu.VMEM((nb * piece, half), low),
             pltpu.VMEM((nw, half, piece), low), pltpu.VMEM((nw, half, piece), low),
             pltpu.VMEM((nb, half, piece), low), pltpu.VMEM((nb, half, piece), low),
             pltpu.VMEM((4, rhs), jnp.float32), pltpu.VMEM((nw * nb, 4, rhs), jnp.float32),
-        ] + sems + [dma((nw,)), dma((nw,)), dma((nb,)), dma((nb,)), dma((1,)), dma((1,))]
+            dma((7,)), dma((nb - 1,)), dma((nw - 1,)), dma((nb // 2,)), dma((7,)),
+        ]
     else:
         body = long_kernel
         scratch = common + [pltpu.VMEM((1, 1), jnp.float32)] + vectors + wide + parts + [

time: 28.3 us -> 26.8 us (0.947)
  Pallas kernels: 26.7 us -> 25.2 us
    pallas_call x1, Pallas kernels: 26 us -> 24.5 us  [on_device(): pl.pallas_call(functools.partial(body, nb, nw), out_shape=(pltpu.VMEM((pi...]
where the time goes in v4:
time: 26.8 us; the launch traced here: 26.5 us
  Pallas kernels  25.2 us (94%)
  between operations  1.28 us (5%)
    pallas_call x1, Pallas kernels, on_device(): pl.pallas_call(functools.partial(body, nb, nw), out_shape=(pltpu.VMEM((pi...  24.5 us
    pallas_call x1, Pallas kernels, on_device(): pl.pallas_call(write_out, out_shape=(jax.ShapeDtypeStruct((piece, rhs), j...  0.77 us

profile of v4, /device:TPU:0, one launch (start us, length us, event | category | flops | bytes accessed | tf_op | source)
XLA Modules:
  0.0 26.5 jit_solution(12175167699577178454)
XLA Ops:
  1.3 24.5 %shard_map.85 = (f32[256,128]{1,0:T(8,128)S(1)}, f32[256,128]{1,0:T(8,128)S(1)}, f32[256,128]{1,0:T(8,128)S(1)}) custom-call(bf16[32,256]{1,0:T(8,128)(2,1)} %bitcast.4, f32[1,32]{1,0:T(1,128)} %bitcast.5, f32[1,1]{1,0:T(1,128)} %bitcast.3.noise_in, f32[256,128]{1,0:T(8,128)} %residual_in.1, f32[256,128]{1,0:T(8,128)} %direction_in.1, f32[256,128]{1,0:T(8,128)} %solution_in.1), custom_call_target="tpu_custom_call" | custom-call | tf_op jit(solution)/shard_map/pallas_call | solution.py:571
  25.7 0.8 %shard_map.86 = (f32[256,128]{1,0:T(8,128)}, f32[256,128]{1,0:T(8,128)}, f32[256,128]{1,0:T(8,128)}) custom-call(f32[256,128]{1,0:T(8,128)S(1)} %get-tuple-element.6.a, f32[256,128]{1,0:T(8,128)S(1)} %get-tuple-element.7.b, f32[256,128]{1,0:T(8,128)S(1)} %get-tuple-element.8.c), custom_call_target="tpu_custom_call" | custom-call | tf_op jit(solution)/shard_map/pallas_call | solution.py:581

commit v5 on v4

--- a/solution.py
+++ b/solution.py
@@ -164,18 +164,23 @@
         tail = jnp.concatenate([norms(block.astype(jnp.float32), 0), ones, blank], axis=0)
         cols_x[slot] = jnp.concatenate([block] * 3 + [tail.astype(jnp.bfloat16)], axis=0)
 
+    start = lax.div(w, nw)
+
+    def stored(j, count=1):
+        return pl.ds(pl.multiple_of((start + j) * piece, piece), count * piece)
+
     def at_rows(j):
         return slice(j * piece, (j + 1) * piece)
 
-    def tiles(rows, slots):
-        for slot in slots:
-            for j in rows:
-                dist = jnp.dot(rows_x[at_rows(j), :], cols_x[slot], preferred_element_type=jnp.float32)
-                kmat[at_rows(j), at_rows(slot)] = matern(dist)
-
     z_near = [0] + z_far[::-1]
 
-    have_rows, have_cols = [], []
+    have_rows, have_cols, due = [], [], []
+
+    def flush():
+        for j, slot in due:
+            dist = jnp.dot(rows_x[at_rows(j), :], cols_x[slot], preferred_element_type=jnp.float32)
+            kmat[at_rows(j), at_rows(slot)] = matern(dist)
+        due.clear()
 
     def add_rows(j):
         if j:
@@ -184,14 +189,16 @@
             make_rows(j, feat_z[q])
         else:
             make_rows(0, feat[0])
-        tiles([j], have_cols)
+        flush()
+        due.extend((j, slot) for slot in have_cols)
         have_rows.append(j)
 
     def add_cols(slot):
         if slot >= chips:
             feat_arrived(slot)
         make_cols(slot)
-        tiles(have_rows, [slot])
+        flush()
+        due.extend((j, slot) for j in have_rows)
         have_cols.append(slot)
 
     every = range(nw)
@@ -199,6 +206,7 @@
     add_rows(0)
     add_cols(0)
     add_cols(chips)
+    flush()
     for q in z_far:
         copy(dir_b.at[0], dir_b.at[nw - q], sent.at[DIR_Z], got.at[DIR_Z], along(q)).start()
     for k in near:
@@ -220,31 +228,33 @@
         add_rows(j)
     for k in last:
         relay_dir(k)
+    for k in last:
+        add_cols(chips + k)
     for k in range(1, chips):
         turn(k)
-    for k in last:
-        add_cols(chips + k)
-
-    def product_a(j):
-        return jnp.dot(kmat[at_rows(j), :], dir_rows[...], preferred_element_type=jnp.float32).T
+    flush()
+
+    def product_a(rows):
+        product = jnp.dot(kmat[stored(rows[0], len(rows)), :], dir_rows[...], preferred_element_type=jnp.float32)
+        return {j: product[at * piece : (at + 1) * piece].T for at, j in enumerate(rows)}
 
     def product_b(slot):
         total = None
         for j in every:
-            term = jnp.dot(dir_b[z_near[j]], kmat[at_rows(j), at_rows(slot)],
+            term = jnp.dot(dir_b[z_near[j]], kmat[stored(j), at_rows(slot)],
                            preferred_element_type=jnp.float32)
             total = term if total is None else total + term
         return total
 
-    def send_a(j):
+    def send_a(j, value):
         q = z_near[j]
-        part_a[j] = product_a(j).astype(jnp.bfloat16)
+        part_a[j] = value.astype(jnp.bfloat16)
         copy(part_a.at[j], part_a_in.at[nw - q], sent.at[PART_Z], got.at[PART_Z], along(q)).start()
 
-    def send_b(k, c):
+    def send_b(k, c, value):
         slot = c * chips + k
         to = (other_chip(k) * 2 + (1 - core if c else core), w)
-        part_b[slot] = product_b(slot).astype(jnp.bfloat16)
+        part_b[slot] = value.astype(jnp.bfloat16)
         copy(part_b.at[slot], part_b_in.at[slot], sent.at[PART], got.at[PART], to).start()
 
     def all_of(ref, kind, recv):
@@ -254,17 +264,25 @@
     all_of(relayed, DIR, dir_sem.at[chips - 1]).wait_recv()
     for k in range(chips):
         turn(chips + k)
-    send_a(nw - 1)
     all_of(z_dirs, DIR_Z, got.at[DIR_Z]).wait_recv()
-    for at_k, k in enumerate(chips_far):
-        for c in range(2):
-            send_b(k, c)
-        if nw - 2 - at_k > 0:
-            send_a(nw - 2 - at_k)
-    for j in range(nw - 1 - len(chips_far) - 1, 0, -1):
-        send_a(j)
-    send_b(0, 1)
-    total_a, total_b = product_a(0), product_b(0)
+    total_a = total_b = None
+    for step in range(max(nw, chips)):
+        j = nw - 1 - step
+        k = (chips_far + [0])[step] if step < chips else None
+        if j >= 0:
+            a = product_a([j])[j]
+        if k is not None:
+            both = [product_b(k), product_b(chips + k)]
+        if j > 0:
+            send_a(j, a)
+        elif j == 0:
+            total_a = a
+        if k:
+            send_b(k, 0, both[0])
+        elif k == 0:
+            total_b = both[0]
+        if k is not None:
+            send_b(k, 1, both[1])
     parts_z, parts_b = part_a_in.at[pl.ds(1, nw - 1)], part_b_in.at[pl.ds(1, nb - 1)]
     all_of(parts_z, PART_Z, got.at[PART_Z]).wait_recv()
     for q in range(1, nw):

time: 26.8 us -> 25.9 us (0.966)
  Pallas kernels: 25.2 us -> 24.3 us
    pallas_call x1, Pallas kernels: 24.5 us -> 23.5 us  [on_device(): pl.pallas_call(functools.partial(body, nb, nw), out_shape=(pltpu.VMEM((pi...]
where the time goes in v5:
time: 25.9 us; the launch traced here: 25.6 us
  Pallas kernels  24.3 us (94%)
  between operations  1.28 us (5%)
    pallas_call x1, Pallas kernels, on_device(): pl.pallas_call(functools.partial(body, nb, nw), out_shape=(pltpu.VMEM((pi...  23.5 us
    pallas_call x1, Pallas kernels, on_device(): pl.pallas_call(write_out, out_shape=(jax.ShapeDtypeStruct((piece, rhs), j...  0.77 us

profile of v5, /device:TPU:0, one launch (start us, length us, event | category | flops | bytes accessed | tf_op | source)
XLA Modules:
  0.0 25.6 jit_solution(8353908190821487246)
XLA Ops:
  1.3 23.5 %shard_map.85 = (f32[256,128]{1,0:T(8,128)S(1)}, f32[256,128]{1,0:T(8,128)S(1)}, f32[256,128]{1,0:T(8,128)S(1)}) custom-call(bf16[32,256]{1,0:T(8,128)(2,1)} %bitcast.4, f32[1,32]{1,0:T(1,128)} %bitcast.5, f32[1,1]{1,0:T(1,128)} %bitcast.3.noise_in, f32[256,128]{1,0:T(8,128)} %residual_in.1, f32[256,128]{1,0:T(8,128)} %direction_in.1, f32[256,128]{1,0:T(8,128)} %solution_in.1), custom_call_target="tpu_custom_call" | custom-call | tf_op jit(solution)/shard_map/pallas_call | solution.py:589
  24.8 0.8 %shard_map.86 = (f32[256,128]{1,0:T(8,128)}, f32[256,128]{1,0:T(8,128)}, f32[256,128]{1,0:T(8,128)}) custom-call(f32[256,128]{1,0:T(8,128)S(1)} %get-tuple-element.6.a, f32[256,128]{1,0:T(8,128)S(1)} %get-tuple-element.7.b, f32[256,128]{1,0:T(8,128)S(1)} %get-tuple-element.8.c), custom_call_target="tpu_custom_call" | custom-call | tf_op jit(solution)/shard_map/pallas_call | solution.py:599

commit v6 on v5

--- a/solution.py
+++ b/solution.py
@@ -8,8 +8,8 @@
 from jax.experimental.pallas import tpu as pltpu
 from jax.sharding import PartitionSpec as P
 
-LN2 = math.log(2.0)
-SCALE = 5.0 / (LN2 * LN2)
+ROOT3 = math.sqrt(3.0)
+SCALE = 5.0 / 3.0
 MESH = pl.DeviceIdType.MESH
 TAIL = 16
 
@@ -28,8 +28,8 @@
 def matern(scaled_dist):
     dist = jnp.maximum(scaled_dist, 1e-30)
     root = dist * lax.rsqrt(dist)
-    poly = 1.0 + root * (LN2 + (LN2 * LN2 / 3.0) * root)
-    return (poly * jnp.exp2(-root)).astype(jnp.bfloat16)
+    poly = root * (root + ROOT3) + 1.0
+    return (poly * jnp.exp2(root * (-ROOT3 / math.log(2.0)))).astype(jnp.bfloat16)
 
 
 def kernel(nb, nw, points_in, inv_in, noise_in, residual_in, direction_in, solution_in, solution_out, residual_out, direction_out,
@@ -71,13 +71,6 @@
     chips_far = sorted(range(1, chips), key=lambda k: -bin(k).count("1"))
     chips_near = chips_far[::-1]
 
-    barrier = pltpu.get_barrier_semaphore()
-    for k in range(1, chips):
-        pl.semaphore_signal(barrier, inc=1, device_id=same_core(k), device_id_type=MESH)
-    pl.semaphore_signal(barrier, inc=1, device_id=sibling, device_id_type=MESH)
-    for q in range(1, nw):
-        pl.semaphore_signal(barrier, inc=1, device_id=along(q), device_id_type=MESH)
-
     def copy(src, dst, send, recv, to):
         return pltpu.make_async_remote_copy(
             src_ref=src, dst_ref=dst, send_sem=send, recv_sem=recv, device_id=to, device_id_type=MESH
@@ -90,7 +83,15 @@
              (residual_in, others.at[0]), (solution_in, others.at[1]))
         )
     ]
-    for load in loads:
+    for load in loads[:2]:
+        load.start()
+    barrier = pltpu.get_barrier_semaphore()
+    for q in z_far:
+        pl.semaphore_signal(barrier, inc=1, device_id=along(q), device_id_type=MESH)
+    for k in chips_far:
+        pl.semaphore_signal(barrier, inc=1, device_id=same_core(k), device_id_type=MESH)
+    pl.semaphore_signal(barrier, inc=1, device_id=sibling, device_id_type=MESH)
+    for load in loads[2:]:
         load.start()
     for load in loads[:2]:
         load.wait()
@@ -102,7 +103,7 @@
     feat[0] = x_t.astype(jnp.bfloat16)
     pl.semaphore_wait(barrier, chips + nw - 1)
 
-    FEAT, FEAT_Z, DIR, DIR_Z, PART, PART_Z, STAT = range(7)
+    DIR_Z, PART, PART_Z, STAT, FEAT, FEAT_Z, DIR = range(7)
 
     def feat_copy(src_slot, dst_slot, to):
         return copy(feat.at[src_slot], feat.at[dst_slot], sent.at[FEAT], feat_sem.at[dst_slot - 1], to)
@@ -115,9 +116,9 @@
 
     for q in z_far:
         feat_z_copy(feat.at[0], nw - q, q).start()
-    for k in chips_far:
+    feat_copy(0, chips, sibling).start()
+    for k in chips_near:
         feat_copy(0, k, same_core(k)).start()
-    feat_copy(0, chips, sibling).start()
     loads[2].wait()
     dir_t = direction[...].T.astype(jnp.bfloat16)
     part = dir_t.shape[0] // 2
@@ -220,14 +221,14 @@
         add_cols(k)
     for k in near:
         add_cols(chips + k)
+    for k in near:
+        relay_dir(k)
     for j in range(2, nw - 1):
         add_rows(j)
-    for k in near:
+    for k in last:
         relay_dir(k)
     for j in range(max(2, nw - 1), nw):
         add_rows(j)
-    for k in last:
-        relay_dir(k)
     for k in last:
         add_cols(chips + k)
     for k in range(1, chips):
@@ -318,7 +319,7 @@
     direction_out[...] = new_residual + new_norm / old_norm * direc
     for ref, kind in ((feat.at[pl.ds(1, nb - 1)], FEAT), (feat_z.at[pl.ds(1, nw - 1)], FEAT_Z), (dir_a.at[pl.ds(1, nb - 1)], DIR),
                       (z_dirs, DIR_Z), (parts_b, PART), (parts_z, PART_Z), (stats, STAT)):
-        all_of(ref, kind, got.at[kind]).wait_send()
+        all_of(ref, kind, got.at[STAT]).wait_send()
 
 
 def long_kernel(nb, nw, points_in, inv_in, noise_in, residual_in, direction_in, solution_in, solution_out, residual_out, direction_out,
@@ -576,7 +577,7 @@
             pltpu.VMEM((nw, half, piece), low), pltpu.VMEM((nw, half, piece), low),
             pltpu.VMEM((nb, half, piece), low), pltpu.VMEM((nb, half, piece), low),
             pltpu.VMEM((4, rhs), jnp.float32), pltpu.VMEM((nw * nb, 4, rhs), jnp.float32),
-            dma((7,)), dma((nb - 1,)), dma((nw - 1,)), dma((nb // 2,)), dma((7,)),
+            dma((7,)), dma((nb - 1,)), dma((nw - 1,)), dma((nb // 2,)), dma((4,)),
         ]
     else:
         body = long_kernel

time: 25.9 us -> 25.1 us (0.969)
  Pallas kernels: 24.3 us -> 23.6 us
    pallas_call x1, Pallas kernels: 23.5 us -> 22.9 us  [on_device(): pl.pallas_call(functools.partial(body, nb, nw), out_shape=(pltpu.VMEM((pi...]
where the time goes in v6:
time: 25.1 us; the launch traced here: 24.9 us
  Pallas kernels  23.6 us (94%)
  between operations  1.28 us (5%)
    pallas_call x1, Pallas kernels, on_device(): pl.pallas_call(functools.partial(body, nb, nw), out_shape=(pltpu.VMEM((pi...  22.9 us
    pallas_call x1, Pallas kernels, on_device(): pl.pallas_call(write_out, out_shape=(jax.ShapeDtypeStruct((piece, rhs), j...  0.77 us

profile of v6, /device:TPU:0, one launch (start us, length us, event | category | flops | bytes accessed | tf_op | source)
XLA Modules:
  0.0 24.9 jit_solution(15411334664783160588)
XLA Ops:
  1.3 22.9 %shard_map.85 = (f32[256,128]{1,0:T(8,128)S(1)}, f32[256,128]{1,0:T(8,128)S(1)}, f32[256,128]{1,0:T(8,128)S(1)}) custom-call(bf16[32,256]{1,0:T(8,128)(2,1)} %bitcast.4, f32[1,32]{1,0:T(1,128)} %bitcast.5, f32[1,1]{1,0:T(1,128)} %bitcast.3.noise_in, f32[256,128]{1,0:T(8,128)} %residual_in.1, f32[256,128]{1,0:T(8,128)} %direction_in.1, f32[256,128]{1,0:T(8,128)} %solution_in.1), custom_call_target="tpu_custom_call" | custom-call | tf_op jit(solution)/shard_map/pallas_call | solution.py:590
  24.1 0.8 %shard_map.86 = (f32[256,128]{1,0:T(8,128)}, f32[256,128]{1,0:T(8,128)}, f32[256,128]{1,0:T(8,128)}) custom-call(f32[256,128]{1,0:T(8,128)S(1)} %get-tuple-element.6.a, f32[256,128]{1,0:T(8,128)S(1)} %get-tuple-element.7.b, f32[256,128]{1,0:T(8,128)S(1)} %get-tuple-element.8.c), custom_call_target="tpu_custom_call" | custom-call | tf_op jit(solution)/shard_map/pallas_call | solution.py:600

commit v7 on v6

--- a/solution.py
+++ b/solution.py
@@ -266,24 +266,21 @@
     for k in range(chips):
         turn(chips + k)
     all_of(z_dirs, DIR_Z, got.at[DIR_Z]).wait_recv()
-    total_a = total_b = None
-    for step in range(max(nw, chips)):
+    for step, k in enumerate(chips_far + [0] + [None] * (nw - chips)):
         j = nw - 1 - step
-        k = (chips_far + [0])[step] if step < chips else None
-        if j >= 0:
-            a = product_a([j])[j]
+        if j > 0:
+            found = product_a([j])[j]
         if k is not None:
-            both = [product_b(k), product_b(chips + k)]
+            pair = [product_b(k), product_b(chips + k)]
         if j > 0:
-            send_a(j, a)
-        elif j == 0:
-            total_a = a
+            send_a(j, found)
         if k:
-            send_b(k, 0, both[0])
+            send_b(k, 0, pair[0])
         elif k == 0:
-            total_b = both[0]
+            total_b = pair[0]
         if k is not None:
-            send_b(k, 1, both[1])
+            send_b(k, 1, pair[1])
+    total_a = product_a([0])[0]
     parts_z, parts_b = part_a_in.at[pl.ds(1, nw - 1)], part_b_in.at[pl.ds(1, nb - 1)]
     all_of(parts_z, PART_Z, got.at[PART_Z]).wait_recv()
     for q in range(1, nw):

time: 25.1 us -> 25.1 us (level)
  no operation moved by 1% of the time
where the time goes in v7:
time: 25.1 us; the launch traced here: 24.9 us
  Pallas kernels  23.6 us (94%)
  between operations  1.28 us (5%)
    pallas_call x1, Pallas kernels, on_device(): pl.pallas_call(functools.partial(body, nb, nw), out_shape=(pltpu.VMEM((pi...  22.9 us
    pallas_call x1, Pallas kernels, on_device(): pl.pallas_call(write_out, out_shape=(jax.ShapeDtypeStruct((piece, rhs), j...  0.77 us

profile of v7, /device:TPU:0, one launch (start us, length us, event | category | flops | bytes accessed | tf_op | source)
XLA Modules:
  0.0 24.9 jit_solution(12167140923224749069)
XLA Ops:
  1.3 22.9 %shard_map.85 = (f32[256,128]{1,0:T(8,128)S(1)}, f32[256,128]{1,0:T(8,128)S(1)}, f32[256,128]{1,0:T(8,128)S(1)}) custom-call(bf16[32,256]{1,0:T(8,128)(2,1)} %bitcast.4, f32[1,32]{1,0:T(1,128)} %bitcast.5, f32[1,1]{1,0:T(1,128)} %bitcast.3.noise_in, f32[256,128]{1,0:T(8,128)} %residual_in.1, f32[256,128]{1,0:T(8,128)} %direction_in.1, f32[256,128]{1,0:T(8,128)} %solution_in.1), custom_call_target="tpu_custom_call" | custom-call | tf_op jit(solution)/shard_map/pallas_call | solution.py:587
  24.1 0.8 %shard_map.86 = (f32[256,128]{1,0:T(8,128)}, f32[256,128]{1,0:T(8,128)}, f32[256,128]{1,0:T(8,128)}) custom-call(f32[256,128]{1,0:T(8,128)S(1)} %get-tuple-element.6.a, f32[256,128]{1,0:T(8,128)S(1)} %get-tuple-element.7.b, f32[256,128]{1,0:T(8,128)S(1)} %get-tuple-element.8.c), custom_call_target="tpu_custom_call" | custom-call | tf_op jit(solution)/shard_map/pallas_call | solution.py:597

commit v8 on v7

--- a/solution.py
+++ b/solution.py
@@ -272,11 +272,11 @@
             found = product_a([j])[j]
         if k is not None:
             pair = [product_b(k), product_b(chips + k)]
+        if k:
+            send_b(k, 0, pair[0])
         if j > 0:
             send_a(j, found)
-        if k:
-            send_b(k, 0, pair[0])
-        elif k == 0:
+        if k == 0:
             total_b = pair[0]
         if k is not None:
             send_b(k, 1, pair[1])

time: 25.1 us -> 25.2 us (level)
  no operation moved by 1% of the time
where the time goes in v8:
time: 25.2 us; the launch traced here: 25 us
  Pallas kernels  23.7 us (94%)
  between operations  1.28 us (5%)
    pallas_call x1, Pallas kernels, on_device(): pl.pallas_call(functools.partial(body, nb, nw), out_shape=(pltpu.VMEM((pi...  22.9 us
    pallas_call x1, Pallas kernels, on_device(): pl.pallas_call(write_out, out_shape=(jax.ShapeDtypeStruct((piece, rhs), j...  0.77 us

profile of v8, /device:TPU:0, one launch (start us, length us, event | category | flops | bytes accessed | tf_op | source)
XLA Modules:
  0.0 25.0 jit_solution(14002547475268896175)
XLA Ops:
  1.3 22.9 %shard_map.85 = (f32[256,128]{1,0:T(8,128)S(1)}, f32[256,128]{1,0:T(8,128)S(1)}, f32[256,128]{1,0:T(8,128)S(1)}) custom-call(bf16[32,256]{1,0:T(8,128)(2,1)} %bitcast.4, f32[1,32]{1,0:T(1,128)} %bitcast.5, f32[1,1]{1,0:T(1,128)} %bitcast.3.noise_in, f32[256,128]{1,0:T(8,128)} %residual_in.1, f32[256,128]{1,0:T(8,128)} %direction_in.1, f32[256,128]{1,0:T(8,128)} %solution_in.1), custom_call_target="tpu_custom_call" | custom-call | tf_op jit(solution)/shard_map/pallas_call | solution.py:587
  24.2 0.8 %shard_map.86 = (f32[256,128]{1,0:T(8,128)}, f32[256,128]{1,0:T(8,128)}, f32[256,128]{1,0:T(8,128)}) custom-call(f32[256,128]{1,0:T(8,128)S(1)} %get-tuple-element.6.a, f32[256,128]{1,0:T(8,128)S(1)} %get-tuple-element.7.b, f32[256,128]{1,0:T(8,128)S(1)} %get-tuple-element.8.c), custom_call_target="tpu_custom_call" | custom-call | tf_op jit(solution)/shard_map/pallas_call | solution.py:597
